TPU v7x, 32 devices: a whole 2x2x4 slice. The times are simulated.
32 devices in a mesh: wave: 8 (over z, y), lev: 4 (over x, core).
Axes of the slice: x: 2, y: 2, z: 4, core: 2. Of those that a mesh axis runs over, the one named last changes fastest.
Arguments:
- spectral: bfloat16 [32, 6, 64, 1280], P('wave', None, 'lev'), may hold values from -0.01171875 to 0.01171875
- legendre: bfloat16 [32, 640, 1280], P('wave'), may hold values from -4 to 4
- wave_ids: int32 [32], replicated, may hold values from 0 to 1279, as said below
- trunc_lengths: int32 [32], replicated, may hold values from 1 to 1280, as said below
- cycle_points: int32 [1280], replicated, may hold values from 20 to 2560, as said below
- grid_coef: float32 [1280, 2560], P('wave'), may hold values from -6 to 6
- cycle_weights: float32 [640], replicated, may hold values from 0.1 to 2
- modes_in: bfloat16 [64, 64], replicated, may hold values from -0.75 to 0.75
- modes_out: bfloat16 [64, 64], replicated, may hold values from -0.75 to 0.75
- depths: float32 [64], replicated, may hold values from 0.05 to 20
Outputs:
- update: bfloat16 [32, 6, 64, 1280], P('wave', None, 'lev')
Inputs may be any that keep to these rules, and one draw needn't show every extreme that they name: `wave_ids`: distinct zonal wavenumbers; one slot holds wavenumber 0. `trunc_lengths`: the length of slot m is at most 1280 minus wave_ids[m] and at least half of that; the slot of wavenumber 0 has length 1280. `cycle_points`: multiples of 4; cycle j and cycle 1280 - 1-j have the same count; cycles near the equator have 2560.
All inputs are finite; a program needn't handle non-finite values.
Results may differ from a plain program's by a relative error of at most 0.011.
Values may be sent and summed in bfloat16 or wider, within the bound.
A program may use at most 128 MiB of HBM per device.

v0:
```python
import functools

import jax
import jax.numpy as jnp
import numpy as np
from jax import lax
from jax.experimental import pallas as pl
from jax.experimental.pallas import tpu as pltpu
from jax.sharding import PartitionSpec as P

NT = 1280
LOW = 256
LANES = 128
GROUP = 8
NN = (((1,), (0,)), ((), ()))
NTD = (((1,), (1,)), ((), ()))
TN = (((0,), (0,)), ((), ()))
F32 = jnp.float32
BF16 = jnp.bfloat16


def turn_coefs(func, degree):
    nodes = 0.125 * (1.0 + np.cos(np.pi * (np.arange(degree + 1) + 0.5) / (degree + 1)))
    cheb = np.polynomial.Chebyshev.fit(nodes, func(nodes), degree, domain=[0.0, 0.25])
    return [float(v) for v in cheb.convert(kind=np.polynomial.Polynomial).coef]


COS = turn_coefs(lambda u: np.cos(2 * np.pi * np.sqrt(u)), 5)
SIN = turn_coefs(lambda u: np.sin(2 * np.pi * np.sqrt(u)) / np.sqrt(u), 5)


def horner(coefs, u):
    total = jnp.full_like(u, coefs[-1])
    for value in coefs[-2::-1]:
        total = total * u + value
    return total


def turns(product, points, inverse):
    return (product - jnp.round(product * inverse) * points) * inverse


def pad_to(value, unit):
    return -(-value // unit) * unit


def join_lanes(pieces, width):
    lane = lax.broadcasted_iota(jnp.int32, pieces[0].shape, 1)
    total = pad_to(len(pieces) * width, LANES) // LANES
    outs = [None] * total
    for no, piece in enumerate(pieces):
        seat, low = divmod(no * width, LANES)
        moved = pltpu.roll(piece, low, 1) if low else piece
        outs[seat] = moved if low == 0 else jnp.where(lane >= low, moved, outs[seat])
        if low + width > LANES:
            outs[seat + 1] = moved
    return jnp.concatenate(outs, axis=1)


def take_lanes(block, no, width):
    seat, low = divmod(no * width, LANES)
    piece = block[:, seat * LANES : (seat + 1) * LANES]
    if low + width > LANES:
        lane = lax.broadcasted_iota(jnp.int32, piece.shape, 1)
        piece = jnp.where(lane >= low, piece, block[:, (seat + 1) * LANES : (seat + 2) * LANES])
    return pltpu.roll(piece, LANES - low, 1) if low else piece


def inverse_kernel(lengths, spec_ref, leg_ref, out_ref, both_ref):
    shards, band, _ = out_ref.shape
    waves, channels, items, span = spec_ref.shape
    rows = channels * items
    wide = both_ref.shape[1] // 2
    part = pl.program_id(0)

    @pl.when(part == 0)
    def _():
        for m in range(waves):
            coeffs = spec_ref[m].reshape(rows, span)
            place = lax.broadcasted_iota(jnp.int32, (rows, span), 1)
            live = jnp.where(place < lengths[m], coeffs.astype(F32), 0.0)
            sign = jnp.where(place % 2 == 0, live, -live).astype(BF16)
            live = live.astype(BF16)
            fill = jnp.zeros((wide - rows, span), BF16)
            both_ref[m] = jnp.concatenate([live, fill, sign, fill], axis=0)

    north, south = [], []
    for m in range(waves):
        sums = lax.dot_general(leg_ref[m], both_ref[m], NTD, preferred_element_type=F32)
        north.append(sums[:, :wide])
        south.append(sums[:, wide:])
    out_ref[part] = join_lanes(north, rows).astype(BF16)
    out_ref[shards - 1 - part] = join_lanes(south, rows).astype(BF16)


def inverse_legendre(spectral, legendre, lengths, shards):
    waves, channels, items, span = spectral.shape
    half_lat = legendre.shape[1]
    band = 2 * half_lat // shards
    rows = channels * items
    lanes = pad_to(waves * rows, LANES)
    wide = pad_to(rows, LANES)
    return pl.pallas_call(
        inverse_kernel,
        name="inverse",
        out_shape=jax.ShapeDtypeStruct((shards, band, lanes), BF16),
        grid_spec=pltpu.PrefetchScalarGridSpec(
            num_scalar_prefetch=1,
            grid=(shards // 2,),
            in_specs=[
                pl.BlockSpec((waves, channels, items, span), lambda k, s: (0, 0, 0, 0)),
                pl.BlockSpec((waves, band, span), lambda k, s: (0, k, 0)),
            ],
            out_specs=pl.BlockSpec((shards, band, lanes), lambda k, s: (0, 0, 0)),
            scratch_shapes=[pltpu.VMEM((waves, 2 * wide, span), BF16)],
        ),
        compiler_params=pltpu.CompilerParams(vmem_limit_bytes=40 << 20),
        cost_estimate=pl.CostEstimate(
            flops=4 * waves * rows * half_lat * span,
            bytes_accessed=2 * waves * half_lat * span,
            transcendentals=0,
        ),
    )(lengths, spectral, legendre)


def forward_kernel(lengths, values_ref, leg_ref, weight_ref, out_ref):
    shards, band, lanes = values_ref.shape
    rows = out_ref.shape[1]
    half = shards // 2
    span = leg_ref.shape[2]
    turn = pl.program_id(0)
    length = lengths[turn]
    seat = turn * rows // LANES
    low = turn * rows % LANES
    after = jnp.minimum(seat + 1, lanes // LANES - 1)

    def side(order):
        here, there = [
            jnp.concatenate([values_ref[k, :, pl.ds(v * LANES, LANES)] for k in order], axis=0)
            for v in (seat, after)
        ]
        lane = lax.broadcasted_iota(jnp.int32, here.shape, 1)
        piece = jnp.where(lane >= low, here.astype(F32), there.astype(F32))
        return pltpu.roll(piece, LANES - low, 1)[:, :rows]

    north = side(range(half))
    south = side([shards - 1 - k for k in range(half)])
    weights = weight_ref[:, :1]
    even = (weights * (north + south)).astype(BF16)
    odd = (weights * (north - south)).astype(BF16)
    polys = leg_ref[0]
    from_even = lax.dot_general(even, polys, TN, preferred_element_type=F32)
    from_odd = lax.dot_general(odd, polys, TN, preferred_element_type=F32)
    place = lax.broadcasted_iota(jnp.int32, (rows, span), 1)
    values = jnp.where(place % 2 == 0, from_even, from_odd)
    out_ref[0] = jnp.where(place < length, values, 0.0).astype(BF16)


def forward_legendre(returned, legendre, lengths, weights, rows):
    shards, band, lanes = returned.shape
    waves, half_lat, span = legendre.shape
    spread = jnp.broadcast_to(weights[:, None], (half_lat, LANES))
    return pl.pallas_call(
        forward_kernel,
        name="forward",
        out_shape=jax.ShapeDtypeStruct((waves, rows, span), BF16),
        grid_spec=pltpu.PrefetchScalarGridSpec(
            num_scalar_prefetch=1,
            grid=(waves,),
            in_specs=[
                pl.BlockSpec((shards, band, lanes), lambda m, s: (0, 0, 0)),
                pl.BlockSpec((1, half_lat, span), lambda m, s: (m, 0, 0)),
                pl.BlockSpec((half_lat, LANES), lambda m, s: (0, 0)),
            ],
            out_specs=pl.BlockSpec((1, rows, span), lambda m, s: (m, 0, 0)),
        ),
        compiler_params=pltpu.CompilerParams(vmem_limit_bytes=40 << 20),
        cost_estimate=pl.CostEstimate(
            flops=4 * waves * rows * half_lat * span,
            bytes_accessed=2 * waves * half_lat * span,
            transcendentals=0,
        ),
    )(lengths, returned, legendre, spread)


def exchange_kernel(
    fields,
    chunk,
    points,
    inverses,
    sent_ref,
    coef_ref,
    lane_ref,
    wave_ref,
    pick_ref,
    merge_ref,
    back_ref,
    land_ref,
    leave_ref,
    in_ref,
    out_ref,
    in_send,
    in_recv,
    out_send,
    out_recv,
    own_sems,
):
    shards, band, _ = sent_ref.shape
    waves = wave_ref.shape[0]
    local_waves = waves // shards
    both_rows = 2 * pick_ref.shape[0]
    rows = both_rows // 2
    items = rows // fields
    lon_max = coef_ref.shape[1]
    chunks = lon_max // LOW
    steps = pad_to(chunks, 8)
    wide = 4 * waves
    me = lax.axis_index("wave")
    reverse = (me * 2) // shards

    barrier = pltpu.get_barrier_semaphore()
    for away in range(1, shards):
        pl.semaphore_signal(
            barrier,
            inc=1,
            device_id={"wave": lax.rem(me + away, shards)},
            device_id_type=pl.DeviceIdType.MESH,
        )
    pl.semaphore_wait(barrier, shards - 1)

    def span_of(part):
        return pl.ds(pl.multiple_of(part * chunk, chunk), chunk)

    def remote(src, dst, send, recv, away, part):
        to = lax.rem(me + away, shards)
        return pltpu.make_async_remote_copy(
            src_ref=src.at[to, span_of(part), :],
            dst_ref=dst.at[me, span_of(part), :],
            send_sem=send.at[away - 1, part],
            recv_sem=recv.at[away - 1, part],
            device_id={"wave": to},
            device_id_type=pl.DeviceIdType.MESH,
        )

    def own(src, dst, which, part):
        return pltpu.make_async_copy(
            src.at[me, span_of(part), :],
            dst.at[me, span_of(part), :],
            own_sems.at[which, part],
        )

    def start_in(part, carry):
        for away in range(1, shards):
            remote(sent_ref, land_ref, in_send, in_recv, away, part).start()
        own(sent_ref, land_ref, 0, part).start()
        return carry

    lax.fori_loop(0, band // chunk, start_in, 0)

    wave_lane = lane_ref[0:1, :]
    step_no = lax.broadcasted_iota(jnp.int32, (steps, wide), 0).astype(F32)
    step_wave = step_no * (wave_lane * float(LOW))
    low_no = lax.broadcasted_iota(jnp.int32, (waves, LANES), 1)
    low_wave = low_no.astype(F32) * wave_ref[...]
    row_lane = lax.broadcasted_iota(jnp.int32, (waves, LANES), 1)
    out_lane = lax.broadcasted_iota(jnp.int32, (rows, 2 * waves), 1)
    place = lax.broadcasted_iota(jnp.int32, (1, LOW), 1).astype(F32)

    def prepare(local):
        pts = points[local]
        inv = inverses[local]
        step = turns(step_wave, pts, inv) - lane_ref[1:2, :]
        step = step - jnp.round(step)
        signs = jnp.where(2.0 * wave_lane < pts, lane_ref[2:3, :], 0.0)
        anal = horner(COS, step * step) * signs
        synth = anal * lane_ref[3:4, :]
        turn = turns(low_wave, pts, inv)
        square = turn * turn
        cos_low = horner(COS, square)
        sin_low = horner(SIN, square) * turn
        half = LANES // 2
        cos_half = jnp.broadcast_to(cos_low[:, half : half + 1], cos_low.shape)
        sin_half = jnp.broadcast_to(sin_low[:, half : half + 1], sin_low.shape)
        twice = cos_half + cos_half
        cos_full = twice * cos_half - 1.0
        sin_full = twice * sin_half
        cos_far = cos_low * cos_full - sin_low * sin_full
        sin_far = sin_low * cos_full + cos_low * sin_full
        cos_all = jnp.concatenate([cos_low.astype(BF16), cos_far.astype(BF16)], axis=1)
        sin_all = jnp.concatenate([sin_low.astype(BF16), sin_far.astype(BF16)], axis=1)
        return pts, inv, synth, anal, cos_all, sin_all

    def pick(seat):
        data = jnp.concatenate(
            [in_ref[w, pl.ds(seat, shards, stride=chunk), :] for w in range(local_waves)], axis=0
        )
        real = jnp.where(row_lane < rows, data, 0.0).astype(BF16)
        other = (row_lane >= rows) & (row_lane < both_rows)
        imag = jnp.where(other, data, 0.0).astype(BF16)
        four = jnp.concatenate([real, imag, imag, real], axis=0)
        spread = lax.dot_general(pick_ref[...], four, NTD, preferred_element_type=F32)
        return spread.astype(BF16)

    def tendency(grid, local, pts):
        pieces = []
        for k in range(chunks):
            vals = grid[k * rows : (k + 1) * rows].astype(BF16)
            after = jnp.concatenate([vals[items:], vals[:items]], axis=0)
            coef = coef_ref[pl.ds(local, 1), k * LOW : (k + 1) * LOW]
            coef = jnp.broadcast_to(coef, (items, LOW)).astype(BF16)
            coef = jnp.concatenate([coef] * fields, axis=0)
            tend = vals * (coef + after)
            live = jnp.broadcast_to(place < pts - float(k * LOW), tend.shape)
            pieces.append(jnp.where(live, tend, jnp.zeros_like(tend)))
        return jnp.concatenate(pieces, axis=0)

    def reduce(back, anal, inv):
        total = back[:rows] * anal[0:1, :]
        for k in range(1, chunks):
            total = total + back[k * rows : (k + 1) * rows] * anal[k : k + 1, :]
        result = (total[:, : 2 * waves] + total[:, 2 * waves :]) * inv
        return jnp.concatenate(
            [
                jnp.where(out_lane < waves, result, 0.0).astype(BF16),
                jnp.where(out_lane < waves, 0.0, result).astype(BF16),
                jnp.zeros((LANES - both_rows, 2 * waves), BF16),
            ],
            axis=0,
        )

    def stretch(row):
        block = jnp.broadcast_to(row, (items, wide)).astype(BF16)
        return jnp.concatenate([block] * fields, axis=0)

    def several(part, step, carry):
        seats = [step * GROUP + g for g in range(GROUP)]
        stored = [part * chunk + v for v in seats]
        locals_ = [v + reverse * (band - 1 - 2 * v) for v in stored]
        made = [prepare(v) for v in locals_]
        spreads = [pick(v) for v in seats]
        turned = [
            jnp.concatenate(
                [x * stretch(w[2][k : k + 1, :]) for k in range(chunks)], axis=0
            )
            for x, w in zip(spreads, made)
        ]
        grids = [
            lax.dot_general(
                x,
                jnp.concatenate([w[4], w[5], w[4], w[5]], axis=0),
                NN,
                preferred_element_type=F32,
            )
            for x, w in zip(turned, made)
        ]
        tends = [tendency(x, v, w[0]) for x, v, w in zip(grids, locals_, made)]
        backs = [
            lax.dot_general(
                x,
                jnp.concatenate([w[4], w[5], w[5], w[4]], axis=0),
                NTD,
                preferred_element_type=F32,
            )
            for x, w in zip(tends, made)
        ]
        splits = [reduce(x, w[3], w[1]) for x, w in zip(backs, made)]
        outs = [
            lax.dot_general(merge_ref[...], x, NTD, preferred_element_type=F32)
            for x in splits
        ]
        for seat, value in zip(seats, outs):
            for w in range(local_waves):
                out_ref[w, pl.ds(seat, shards, stride=chunk), :] = value[w * shards : (w + 1) * shards]
        return carry

    def work(part, carry):
        for away in range(1, shards):
            remote(sent_ref, land_ref, in_send, in_recv, away, part).wait_recv()
        own(sent_ref, land_ref, 0, part).wait()
        got = land_ref[:, span_of(part), :].astype(F32).reshape(shards * chunk, -1)
        for w in range(local_waves):
            in_ref[w] = take_lanes(got, w, both_rows)
        lax.fori_loop(0, chunk // GROUP, functools.partial(several, part), 0)
        made = join_lanes([out_ref[w] for w in range(local_waves)], both_rows).astype(BF16)
        leave_ref[:, span_of(part), :] = made.reshape(shards, chunk, -1)
        for away in range(1, shards):
            remote(leave_ref, back_ref, out_send, out_recv, away, part).start()
        own(leave_ref, back_ref, 1, part).start()
        return carry

    lax.fori_loop(0, band // chunk, work, 0)

    def finish(part, carry):
        for away in range(1, shards):
            remote(sent_ref, land_ref, in_send, in_recv, away, part).wait_send()
            remote(leave_ref, back_ref, out_send, out_recv, away, part).wait()
        own(leave_ref, back_ref, 1, part).wait()
        return carry

    lax.fori_loop(0, band // chunk, finish, 0)


def cycle_trips(values, wave_ids, points, coef, fields, both_rows):
    shards, band, _ = values.shape
    waves = wave_ids.shape[0]
    local_waves = waves // shards
    rows = both_rows // 2
    wide = 4 * waves
    lon_max = coef.shape[1]
    chunk = next(c for c in (16, 8) if band % c == 0)
    parts = band // chunk
    wave_ids = wave_ids.reshape(shards, local_waves).T.reshape(-1)
    lane = jnp.arange(wide)
    part = lane // waves
    wave_lane = jnp.tile(wave_ids, 4).astype(F32)
    factor = jnp.where(wave_lane == 0, 1.0, 2.0)
    quarter = jnp.where(part < 2, 0.0, 0.25)
    signs = jnp.where(part == 0, 1.0, -1.0)
    zero = jnp.zeros_like(factor)
    lanes = jnp.stack([wave_lane, quarter, signs, factor, zero, zero, zero, zero], axis=0)
    wave_col = jnp.broadcast_to(wave_ids.astype(F32)[:, None], (waves, LANES))
    lanes_in = jnp.arange(LANES)[None, :]
    pick = (jnp.arange(rows)[:, None] == lanes_in % rows) & (lanes_in < both_rows)
    pick = pick.astype(BF16)
    merge = (jnp.arange(waves)[:, None] == jnp.arange(2 * waves)[None, :] % waves).astype(BF16)

    vmem = pl.BlockSpec(memory_space=pltpu.VMEM)
    smem = pl.BlockSpec(memory_space=pltpu.SMEM)
    dma = pltpu.SemaphoreType.DMA
    return pl.pallas_call(
        functools.partial(exchange_kernel, fields, chunk),
        name="cycles",
        out_shape=jax.ShapeDtypeStruct(values.shape, BF16),
        in_specs=[smem, smem] + [vmem] * 6,
        out_specs=vmem,
        scratch_shapes=[
            pltpu.VMEM(values.shape, BF16),
            pltpu.VMEM(values.shape, BF16),
            pltpu.VMEM((local_waves, shards * chunk, LANES), F32),
            pltpu.VMEM((local_waves, shards * chunk, LANES), F32),
            dma((shards - 1, parts)),
            dma((shards - 1, parts)),
            dma((shards - 1, parts)),
            dma((shards - 1, parts)),
            dma((2, parts)),
        ],
        compiler_params=pltpu.CompilerParams(
            vmem_limit_bytes=30 << 20, collective_id=0, has_side_effects=True
        ),
        cost_estimate=pl.CostEstimate(
            flops=8 * band * waves * rows * lon_max,
            bytes_accessed=4 * band * lon_max,
            transcendentals=0,
        ),
    )(
        points.astype(F32),
        1.0 / points.astype(F32),
        values,
        coef,
        lanes,
        wave_col,
        pick,
        merge,
    )


def level_kernel(
    channels,
    levs,
    ids,
    own_ref,
    in_ref,
    out_modes_ref,
    depth_ref,
    update_ref,
    all_ref,
    far_send,
    far_recv,
    near_send,
    near_recv,
    own_sems,
):
    waves, rows, span = own_ref.shape
    items = rows // channels
    modes = in_ref.shape[0]
    chips = levs // 2
    me = lax.axis_index("lev")
    chip, core = me // 2, lax.rem(me, 2)
    partner = chip * 2 + 1 - core

    barrier = pltpu.get_barrier_semaphore()
    peers = [lax.rem(chip + d, chips) * 2 + core for d in range(1, chips)]
    for peer in peers + [partner]:
        pl.semaphore_signal(
            barrier, inc=1, device_id={"lev": peer}, device_id_type=pl.DeviceIdType.MESH
        )
    pl.semaphore_wait(barrier, chips)

    def far(away, m):
        return pltpu.make_async_remote_copy(
            src_ref=own_ref.at[m],
            dst_ref=all_ref.at[me, m],
            send_sem=far_send.at[away - 1, m],
            recv_sem=far_recv.at[away - 1, m],
            device_id={"lev": peers[away - 1]},
            device_id_type=pl.DeviceIdType.MESH,
        )

    def near(away, m):
        owner = lax.rem(chip + chips - away, chips) * 2 + core
        return pltpu.make_async_remote_copy(
            src_ref=own_ref.at[m] if away == 0 else all_ref.at[owner, m],
            dst_ref=all_ref.at[owner, m],
            send_sem=near_send.at[away, m],
            recv_sem=near_recv.at[away, m],
            device_id={"lev": partner},
            device_id_type=pl.DeviceIdType.MESH,
        )

    def own(m):
        return pltpu.make_async_copy(own_ref.at[m], all_ref.at[me, m], own_sems.at[m])

    for m in range(waves):
        for away in range(1, chips):
            far(away, m).start()
        near(0, m).start()
        own(m).start()

    def solve(m):
        own(m).wait()
        for away in range(chips):
            near(away, m).wait_recv()
        place = lax.broadcasted_iota(jnp.int32, (modes, span), 1)
        degree = (place + ids[m]).astype(F32)
        damp = 1.0 / (1.0 + depth_ref[:, :1] * degree * (degree + 1.0) / float(NT * NT))
        for c in range(channels):
            stack = jnp.concatenate(
                [all_ref[s, m, c * items : (c + 1) * items, :] for s in range(levs)], axis=0
            )
            vals = lax.dot_general(in_ref[...], stack, NN, preferred_element_type=F32)
            scaled = (vals * damp).astype(BF16)
            update_ref[m, c] = lax.dot_general(
                out_modes_ref[...], scaled, NN, preferred_element_type=F32
            ).astype(BF16)

    for m in range(waves):
        for away in range(1, chips):
            far(away, m).wait_recv()
            near(away, m).start()
        if m > 0:
            solve(m - 1)
    solve(waves - 1)
    for m in range(waves):
        for away in range(1, chips):
            far(away, m).wait_send()
        for away in range(chips):
            near(away, m).wait_send()


def vertical(projected, modes_in, own_rows, depths, own_waves, channels, levs):
    waves, rows, span = projected.shape
    items = rows // channels
    modes = modes_in.shape[0]
    chips = levs // 2
    spread = jnp.broadcast_to(depths[:, None], (modes, LANES))
    vmem = pl.BlockSpec(memory_space=pltpu.VMEM)
    dma = pltpu.SemaphoreType.DMA
    return pl.pallas_call(
        functools.partial(level_kernel, channels, levs),
        name="vertical",
        out_shape=jax.ShapeDtypeStruct((waves, channels, items, span), BF16),
        in_specs=[pl.BlockSpec(memory_space=pltpu.SMEM)] + [vmem] * 4,
        out_specs=vmem,
        scratch_shapes=[
            pltpu.VMEM((levs, waves, rows, span), BF16),
            dma((max(chips - 1, 1), waves)),
            dma((max(chips - 1, 1), waves)),
            dma((chips, waves)),
            dma((chips, waves)),
            dma((waves,)),
        ],
        compiler_params=pltpu.CompilerParams(
            vmem_limit_bytes=40 << 20, collective_id=1, has_side_effects=True
        ),
    )(own_waves, projected, modes_in, own_rows, spread)


def on_device(
    spectral,
    legendre,
    wave_ids,
    trunc_lengths,
    cycle_points,
    grid_coef,
    cycle_weights,
    modes_in,
    modes_out,
    depths,
):
    wave_rank = lax.axis_index("wave")
    lev_rank = lax.axis_index("lev")
    shards = lax.axis_size("wave")
    waves, channels, items, span = spectral.shape
    rows = channels * items
    band = grid_coef.shape[0]
    own_waves = lax.dynamic_slice_in_dim(wave_ids, wave_rank * waves, waves)
    own_lengths = lax.dynamic_slice_in_dim(trunc_lengths, wave_rank * waves, waves)
    fourier = inverse_legendre(spectral, legendre, own_lengths, shards)
    points = lax.dynamic_slice_in_dim(cycle_points, wave_rank * band, band)
    returned = cycle_trips(fourier, wave_ids, points, grid_coef, channels // 2, rows)
    projected = forward_legendre(returned, legendre, own_lengths, cycle_weights, rows)
    own_rows = lax.dynamic_slice_in_dim(modes_out, lev_rank * items, items, 0)
    levs = lax.axis_size("lev")
    return vertical(projected, modes_in, own_rows, depths, own_waves, channels, levs)


def solution(mesh):
    placed = (
        P("wave", None, "lev", None),
        P("wave", None, None),
        P(),
        P(),
        P(),
        P("wave", None),
        P(),
        P(),
        P(),
        P(),
    )
    return jax.shard_map(
        on_device,
        mesh=mesh,
        in_specs=placed,
        out_specs=P("wave", None, "lev", None),
        check_vma=False,
    )
```

profile of v0, /device:TPU:0, one launch (start us, length us, event | category | flops | bytes accessed | tf_op | source)
XLA Modules:
  0.0 99.6 jit_solution(11910084623478595016)
XLA Ops:
  0.0 0.0 copy-start
  0.0 0.0 copy-start.8
  0.0 0.8 dynamic_slice.13.lengths
  0.8 0.0 copy-start.1
  0.8 2.9 %copy-done.1 = bf16[4,640,1280]{2,1,0:T(8,128)(2,1)S(1)} copy-done((bf16[4,640,1280]{2,1,0:T(8,128)(2,1)S(1)}, bf16[4,640,1280]{2,1,0:T(8,128)(2,1)}, u32[]{:S(2)}) %copy-start.1) | copy-done | bytes 6553624
  3.6 0.0 copy-start.3
  3.6 1.2 %copy-done.3 = bf16[4,6,16,1280]{3,2,1,0:T(8,128)(2,1)S(1)} copy-done((bf16[4,6,16,1280]{3,2,1,0:T(8,128)(2,1)S(1)}, bf16[4,6,16,1280]{3,2,1,0:T(8,128)(2,1)}, u32[]{:S(2)}) %copy-start.3) | copy-done | bytes 983064
  4.8 0.0 copy-start.5
  4.8 5.8 %inverse.1.sent_ref = bf16[8,160,384]{2,1,0:T(8,128)(2,1)S(1)} custom-call(s32[4]{0:T(128)S(1)} %dynamic_slice.13.lengths, bf16[4,6,16,1280]{3,2,1,0:T(8,128)(2,1)S(1)} %copy-done.3, bf16[4,640,1280]{2,1,0:T(8,128)(2,1)S(1)} %copy-done.1), custom_call_target="tpu_custom_call" | custom-call | flops 1258291200 | bytes 6553600 | tf_op jit(solution)/shard_map/inverse/pallas_call | solution.py:103
  10.6 0.8 broadcast_divide_fusion
  11.4 0.0 copy-done.8
  11.4 0.1 convert_element_type.47
  11.5 0.1 copy.12
  11.5 0.1 convert_element_type.49
  11.6 0.1 convert_element_type.50
  11.8 0.1 broadcast_in_dim.45.wave_ref
  11.9 0.0 copy-done.5
  11.9 0.0 copy-start.6
  11.9 0.0 copy-start.2
  12.0 54.8 %cycles.1.values_ref = bf16[8,160,384]{2,1,0:T(8,128)(2,1)S(1)} custom-call(f32[160]{0:T(256)S(1)} %get-tuple-element.6.points, f32[160]{0:T(256)S(1)} %get-tuple-element.5.inverses, bf16[8,160,384]{2,1,0:T(8,128)(2,1)S(1)} %inverse.1.sent_ref, f32[160,2560]{1,0:T(8,128)S(1)} %copy-done.5, f32[8,128]{1,0:T(8,128)S(1)} %stack.5.lane_ref, ...), custom_call_target="tpu_custom_call" | custom-call | flops 5033164800 | bytes 1638400 | tf_op jit(solution)/shard_map/cycles/pallas_call | solution.py:430
  66.8 0.0 copy-done.6
  66.8 0.0 copy-start.7
  66.8 0.0 copy-start.4
  66.8 0.1 broadcast_in_dim.46.weight_ref
  67.0 0.0 copy-done.2
  67.0 4.4 %forward.1.own_ref = bf16[4,96,1280]{2,1,0:T(8,128)(2,1)S(1)} custom-call(s32[4]{0:T(128)S(1)} %dynamic_slice.13.lengths, bf16[8,160,384]{2,1,0:T(8,128)(2,1)S(1)} %cycles.1.values_ref, bf16[4,640,1280]{2,1,0:T(8,128)(2,1)S(1)} %copy-done.2, f32[640,128]{1,0:T(8,128)S(1)} %broadcast_in_dim.46.weight_ref), custom_call_target="tpu_custom_call" | custom-call | flops 1258291200 | bytes 6553600 | tf_op jit(solution)/shard_map/forward/pallas_call | solution.py:163
  71.4 0.1 dynamic_slice.12.ids
  71.5 0.0 copy-done
  71.5 0.0 copy-done.7
  71.5 0.1 broadcast_in_dim.47.depth_ref
  71.6 0.0 copy-done.4
  71.6 27.1 %vertical.1 = bf16[4,6,16,1280]{3,2,1,0:T(8,128)(2,1)S(1)} custom-call(s32[4]{0:T(128)S(1)} %dynamic_slice.12.ids, bf16[4,96,1280]{2,1,0:T(8,128)(2,1)S(1)} %forward.1.own_ref, bf16[64,64]{1,0:T(8,128)(2,1)S(1)} %copy-done.4, bf16[16,64]{1,0:T(8,128)(2,1)S(1)} %constant_dynamic-slice_fusion.out_modes_ref, f32[64,128]{1,0:T(8,128)S(1)} %broadcast_in_dim.47.depth_ref), custom_call_target="tpu_custom_call" | custom-call | tf_op jit(solution)/shard_map/vertical/pallas_call | solution.py:568
  98.7 0.9 copy.14
  (12 shorter events, 0.1 us)
Async XLA Ops:
  0.0 71.5 %copy-start = (bf16[64,64]{1,0:T(8,128)(2,1)S(1)}, bf16[64,64]{1,0:T(8,128)(2,1)}, u32[]{:S(2)}) copy-start(bf16[64,64]{1,0:T(8,128)(2,1)} %param.18) | copy-start | bytes 24580
  0.0 11.4 %copy-start.8 = (s32[32]{0:T(128)S(1)}, s32[32]{0:T(128)}, u32[]{:S(2)}) copy-start(s32[32]{0:T(128)} %param.12) | copy-start | bytes 388
  0.8 2.9 %copy-start.1 = (bf16[4,640,1280]{2,1,0:T(8,128)(2,1)S(1)}, bf16[4,640,1280]{2,1,0:T(8,128)(2,1)}, u32[]{:S(2)}) copy-start(bf16[4,640,1280]{2,1,0:T(8,128)(2,1)} %leg_ref.3) | copy-start | bytes 19660804
  3.6 1.2 %copy-start.3 = (bf16[4,6,16,1280]{3,2,1,0:T(8,128)(2,1)S(1)}, bf16[4,6,16,1280]{3,2,1,0:T(8,128)(2,1)}, u32[]{:S(2)}) copy-start(bf16[4,6,16,1280]{3,2,1,0:T(8,128)(2,1)} %spec_ref.1) | copy-start | bytes 2949124
  4.8 7.1 %copy-start.5 = (f32[160,2560]{1,0:T(8,128)S(1)}, f32[160,2560]{1,0:T(8,128)}, u32[]{:S(2)}) copy-start(f32[160,2560]{1,0:T(8,128)} %coef_ref.1) | copy-start | bytes 4915204
  11.9 54.9 %copy-start.6 = (f32[640]{0:T(1024)S(1)}, f32[640]{0:T(1024)}, u32[]{:S(2)}) copy-start(f32[640]{0:T(1024)} %param.16) | copy-start | bytes 7684
  11.9 55.0 %copy-start.2 = (bf16[4,640,1280]{2,1,0:T(8,128)(2,1)S(1)}, bf16[4,640,1280]{2,1,0:T(8,128)(2,1)}, u32[]{:S(2)}) copy-start(bf16[4,640,1280]{2,1,0:T(8,128)(2,1)} %leg_ref.3) | copy-start | bytes 19660804
  66.8 4.7 %copy-start.7 = (f32[64]{0:T(128)S(1)}, f32[64]{0:T(128)}, u32[]{:S(2)}) copy-start(f32[64]{0:T(128)} %param.19) | copy-start | bytes 772
  66.8 4.8 %copy-start.4 = (bf16[64,64]{1,0:T(8,128)(2,1)S(1)}, bf16[64,64]{1,0:T(8,128)(2,1)}, u32[]{:S(2)}) copy-start(bf16[64,64]{1,0:T(8,128)(2,1)} %in_ref.1) | copy-start | bytes 24580
where the time goes:
time: 99.9 us; the launch traced here: 99.6 us
  Pallas kernels  92.1 us (92%)
  local copies, waits for them, and re-layouts  6.53 us (7%)
    pallas_call x1, Pallas kernels, cycle_trips(): pl.pallas_call(functools.partial(exchange_kernel, fields, chunk), name='c...  54.8 us
    pallas_call x1, Pallas kernels, vertical(): pl.pallas_call(functools.partial(level_kernel, channels, levs), name='ver...  27.1 us
    pallas_call x1, Pallas kernels, inverse_legendre(): pl.pallas_call(inverse_kernel, name='inverse', out_shape=jax.ShapeDtypeSt...  5.76 us
    unnamed x19, local copies, waits for them, and re-layouts  5.04 us
    pallas_call x1, Pallas kernels, forward_legendre(): pl.pallas_call(forward_kernel, name='forward', out_shape=jax.ShapeDtypeSt...  4.44 us

commit v1 on v0

v1 whole, which is shorter than its diff:
```python
import functools

import jax
import jax.numpy as jnp
import numpy as np
from jax import lax
from jax.experimental import pallas as pl
from jax.experimental.pallas import tpu as pltpu
from jax.sharding import PartitionSpec as P

NT = 1280
LOW = 256
LANES = 128
GROUP = 8
LEAD = 2
FIRST = 3
SECOND = 5
NN = (((1,), (0,)), ((), ()))
NTD = (((1,), (1,)), ((), ()))
F32 = jnp.float32
BF16 = jnp.bfloat16


def turn_coefs(func, degree):
    nodes = 0.125 * (1.0 + np.cos(np.pi * (np.arange(degree + 1) + 0.5) / (degree + 1)))
    cheb = np.polynomial.Chebyshev.fit(nodes, func(nodes), degree, domain=[0.0, 0.25])
    return [float(v) for v in cheb.convert(kind=np.polynomial.Polynomial).coef]


COS = turn_coefs(lambda u: np.cos(2 * np.pi * np.sqrt(u)), 5)
SIN = turn_coefs(lambda u: np.sin(2 * np.pi * np.sqrt(u)) / np.sqrt(u), 5)


def horner(coefs, u):
    total = jnp.full_like(u, coefs[-1])
    for value in coefs[-2::-1]:
        total = total * u + value
    return total


def turns(product, points, inverse):
    return (product - jnp.round(product * inverse) * points) * inverse


def pad_to(value, unit):
    return -(-value // unit) * unit


def join_lanes(pieces, width):
    lane = lax.broadcasted_iota(jnp.int32, pieces[0].shape, 1)
    total = pad_to(len(pieces) * width, LANES) // LANES
    outs = [None] * total
    for no, piece in enumerate(pieces):
        seat, low = divmod(no * width, LANES)
        moved = pltpu.roll(piece, low, 1) if low else piece
        outs[seat] = moved if low == 0 else jnp.where(lane >= low, moved, outs[seat])
        if low + width > LANES:
            outs[seat + 1] = moved
    return jnp.concatenate(outs, axis=1)


def take_lanes(block, no, width):
    seat, low = divmod(no * width, LANES)
    piece = block[:, seat * LANES : (seat + 1) * LANES]
    if low + width > LANES:
        lane = lax.broadcasted_iota(jnp.int32, piece.shape, 1)
        piece = jnp.where(lane >= low, piece, block[:, (seat + 1) * LANES : (seat + 2) * LANES])
    return pltpu.roll(piece, LANES - low, 1) if low else piece


def trip_kernel(
    chunk,
    stride,
    all_ids,
    all_lengths,
    all_points,
    spec_hbm,
    leg_hbm,
    coef_hbm,
    weight_row,
    in_modes_ref,
    out_modes_ref,
    depth_row,
    update_ref,
    spec_ref,
    leg_ref,
    coef_ref,
    both_ref,
    sent_ref,
    land_ref,
    leave_ref,
    all_ref,
    in_ref,
    out_ref,
    turned_ref,
    give_ref,
    weight_ref,
    depth_ref,
    spec_sem,
    leg_sems,
    coef_sem,
    in_send,
    in_recv,
    out_send,
    out_recv,
    far_send,
    far_recv,
    near_send,
    near_recv,
    own_sems,
    give_send,
    give_recv,
):
    shards, band, lanes = sent_ref.shape
    levs = all_ref.shape[0]
    local_waves, channels, items, span = spec_ref.shape
    half_lat = leg_ref.shape[1]
    half = shards // 2
    fields = channels // 2
    both_rows = channels * items
    rows = both_rows // 2
    padded = both_ref.shape[1] // 2
    waves = shards * local_waves
    lon_max = coef_ref.shape[1]
    chunks = lon_max // LOW
    steps = pad_to(chunks, 8)
    wide = 4 * waves
    modes = in_modes_ref.shape[0]
    parts = band // chunk
    chips = levs // 2
    me = lax.axis_index("wave")
    lev = lax.axis_index("lev")
    reverse = (me * 2) // shards
    chip, core = lev // 2, lax.rem(lev, 2)
    partner = chip * 2 + 1 - core
    peers = [lax.rem(chip + d, chips) * 2 + core for d in range(1, chips)]

    spec_copy = pltpu.make_async_copy(spec_hbm, spec_ref, spec_sem)
    coef_copy = pltpu.make_async_copy(coef_hbm, coef_ref, coef_sem)

    def leg_copy(step, k):
        where = pl.ds(pl.multiple_of(k * band + step * stride, 8), stride)
        return pltpu.make_async_copy(
            leg_hbm.at[:, where, :], leg_ref.at[:, where, :], leg_sems.at[step, k]
        )

    spec_copy.start()

    def start_leg(step, carry):
        for k in range(half):
            leg_copy(step, k).start()
        return carry

    lax.fori_loop(0, band // stride, start_leg, 0)
    coef_copy.start()

    barrier = pltpu.get_barrier_semaphore()
    for away in range(1, shards):
        pl.semaphore_signal(
            barrier,
            inc=1,
            device_id={"wave": lax.rem(me + away, shards)},
            device_id_type=pl.DeviceIdType.MESH,
        )
    for peer in peers + [partner]:
        pl.semaphore_signal(
            barrier, inc=1, device_id={"lev": peer}, device_id_type=pl.DeviceIdType.MESH
        )

    def span_of(part):
        return pl.ds(pl.multiple_of(part * chunk, chunk), chunk)

    def remote(src, dst, send, recv, away, part):
        to = lax.rem(me + away, shards)
        return pltpu.make_async_remote_copy(
            src_ref=src.at[to, span_of(part), :],
            dst_ref=dst.at[me, span_of(part), :],
            send_sem=send.at[away - 1, part],
            recv_sem=recv.at[away - 1, part],
            device_id={"wave": to},
            device_id_type=pl.DeviceIdType.MESH,
        )

    def own(src, dst, which, part):
        return pltpu.make_async_copy(
            src.at[me, span_of(part), :],
            dst.at[me, span_of(part), :],
            own_sems.at[which, part],
        )

    back_ref = all_ref.at[lev]

    def far(away, part):
        return pltpu.make_async_remote_copy(
            src_ref=all_ref.at[lev, :, span_of(part), :],
            dst_ref=all_ref.at[lev, :, span_of(part), :],
            send_sem=far_send.at[away - 1, part],
            recv_sem=far_recv.at[away - 1, part],
            device_id={"lev": peers[away - 1]},
            device_id_type=pl.DeviceIdType.MESH,
        )

    def near(away, part):
        owner = lax.rem(chip + chips - away, chips) * 2 + core
        return pltpu.make_async_remote_copy(
            src_ref=all_ref.at[owner, :, span_of(part), :],
            dst_ref=all_ref.at[owner, :, span_of(part), :],
            send_sem=near_send.at[away, part],
            recv_sem=near_recv.at[away, part],
            device_id={"lev": partner},
            device_id_type=pl.DeviceIdType.MESH,
        )

    def pass_far(part):
        for away in range(1, shards):
            remote(leave_ref, back_ref, out_send, out_recv, away, part).wait_recv()
        own(leave_ref, back_ref, 1, part).wait()
        for away in range(1, chips):
            far(away, part).start()
        near(0, part).start()

    def pass_near(part):
        for away in range(1, chips):
            far(away, part).wait_recv()
            near(away, part).start()

    def start_in(part, carry):
        for away in range(1, shards):
            remote(sent_ref, land_ref, in_send, in_recv, away, part).start()
        own(sent_ref, land_ref, 0, part).start()
        return carry

    spec_copy.wait()
    for m in range(local_waves):
        coeffs = spec_ref[m].reshape(both_rows, span)
        seat = lax.broadcasted_iota(jnp.int32, (both_rows, span), 1)
        live = jnp.where(seat < all_lengths[me * local_waves + m], coeffs.astype(F32), 0.0)
        sign = jnp.where(seat % 2 == 0, live, -live).astype(BF16)
        fill = jnp.zeros((padded - both_rows, span), BF16)
        both_ref[m] = jnp.concatenate([live.astype(BF16), fill, sign, fill], axis=0)

    def inverse(step):
        for k in range(half):
            leg_copy(step, k).wait()
        north, south = [], []
        for m in range(local_waves):
            polys = jnp.concatenate(
                [
                    leg_ref[m, pl.ds(pl.multiple_of(k * band + step * stride, 8), stride), :]
                    for k in range(half)
                ],
                axis=0,
            )
            sums = lax.dot_general(polys, both_ref[m], NTD, preferred_element_type=F32)
            north.append(sums[:, :padded])
            south.append(sums[:, padded:])
        north = join_lanes(north, both_rows).astype(BF16)
        south = join_lanes(south, both_rows).astype(BF16)
        where = pl.ds(pl.multiple_of(step * stride, 8), stride)
        for k in range(half):
            sent_ref[k, where, :] = north[k * stride : (k + 1) * stride]
            sent_ref[shards - 1 - k, where, :] = south[k * stride : (k + 1) * stride]

    each = stride // chunk

    def more(step, carry):
        inverse(step)

        @pl.when(step == 0)
        def _():
            pl.semaphore_wait(barrier, shards - 1 + chips)

        for e in range(each):

            @pl.when(step * each + e < LEAD)
            def _():
                start_in(step * each + e, 0)

        return carry

    lax.fori_loop(0, band // stride, more, 0)
    coef_copy.wait()
    for v in range(weight_row.shape[0]):
        row = weight_row[v : v + 1, :]
        weight_ref[v * LANES : (v + 1) * LANES, :] = jnp.broadcast_to(row, (LANES, LANES)).T
    depth_ref[...] = jnp.broadcast_to(depth_row[...], (LANES, modes)).T

    lane = lax.broadcasted_iota(jnp.int32, (1, wide), 1)
    slot = lane % waves
    wave_lane = jnp.zeros((1, wide), F32)
    columns = []
    for w in range(local_waves):
        for s in range(shards):
            value = all_ids[s * local_waves + w].astype(F32)
            wave_lane = jnp.where(slot == w * shards + s, value, wave_lane)
            columns.append(jnp.full((1, LANES), value, F32))
    wave_col = jnp.concatenate(columns, axis=0)
    quarter = jnp.where(lane < 2 * waves, 0.0, 0.25)
    all_signs = jnp.where(lane < waves, 1.0, -1.0)
    factor = jnp.where(wave_lane == 0.0, 1.0, 2.0)
    step_no = lax.broadcasted_iota(jnp.int32, (steps, wide), 0).astype(F32)
    step_wave = step_no * (wave_lane * float(LOW))
    low_no = lax.broadcasted_iota(jnp.int32, (waves, LANES), 1)
    low_wave = low_no.astype(F32) * wave_col
    row_lane = lax.broadcasted_iota(jnp.int32, (waves, LANES), 1)
    out_lane = lax.broadcasted_iota(jnp.int32, (rows, 2 * waves), 1)
    place = lax.broadcasted_iota(jnp.int32, (1, LOW), 1).astype(F32)
    pick_row = lax.broadcasted_iota(jnp.int32, (rows, LANES), 0)
    pick_lane = lax.broadcasted_iota(jnp.int32, (rows, LANES), 1)
    picks = ((pick_lane == pick_row) | (pick_lane == pick_row + rows)).astype(F32).astype(BF16)
    merge_row = lax.broadcasted_iota(jnp.int32, (waves, 2 * waves), 0)
    merge_lane = lax.broadcasted_iota(jnp.int32, (waves, 2 * waves), 1)
    merges = (merge_lane % waves == merge_row).astype(F32).astype(BF16)

    def prepare(local):
        count = all_points[me * band + local].astype(F32)
        pts = jnp.full((1, wide), count, F32)
        inv = 1.0 / pts
        step = turns(step_wave, pts, inv) - quarter
        step = step - jnp.round(step)
        signs = jnp.where(2.0 * wave_lane < count, all_signs, 0.0)
        anal = horner(COS, step * step) * signs
        synth = anal * factor
        turn = turns(low_wave, pts[:, :LANES], inv[:, :LANES])
        square = turn * turn
        cos_low = horner(COS, square)
        sin_low = horner(SIN, square) * turn
        mid = LANES // 2
        cos_half = jnp.broadcast_to(cos_low[:, mid : mid + 1], cos_low.shape)
        sin_half = jnp.broadcast_to(sin_low[:, mid : mid + 1], sin_low.shape)
        twice = cos_half + cos_half
        cos_full = twice * cos_half - 1.0
        sin_full = twice * sin_half
        cos_far = cos_low * cos_full - sin_low * sin_full
        sin_far = sin_low * cos_full + cos_low * sin_full
        cos_all = jnp.concatenate([cos_low.astype(BF16), cos_far.astype(BF16)], axis=1)
        sin_all = jnp.concatenate([sin_low.astype(BF16), sin_far.astype(BF16)], axis=1)
        return count, inv[:, : 2 * waves], synth, anal, cos_all, sin_all

    def pick(seat):
        data = jnp.concatenate(
            [in_ref[w, pl.ds(seat, shards, stride=chunk), :] for w in range(local_waves)], axis=0
        )
        real = jnp.where(row_lane < rows, data, 0.0).astype(BF16)
        other = (row_lane >= rows) & (row_lane < both_rows)
        imag = jnp.where(other, data, 0.0).astype(BF16)
        four = jnp.concatenate([real, imag, imag, real], axis=0)
        spread = lax.dot_general(picks, four, NTD, preferred_element_type=F32)
        return spread.astype(BF16)

    def tendency(grid, local, pts):
        pieces = []
        for k in range(chunks):
            vals = grid[k * rows : (k + 1) * rows].astype(BF16)
            after = jnp.concatenate([vals[items:], vals[:items]], axis=0)
            coef = coef_ref[pl.ds(local, 1), k * LOW : (k + 1) * LOW]
            coef = jnp.broadcast_to(coef, (items, LOW)).astype(BF16)
            coef = jnp.concatenate([coef] * fields, axis=0)
            tend = vals * (coef + after)
            live = jnp.broadcast_to(place < pts - float(k * LOW), tend.shape)
            pieces.append(jnp.where(live, tend, jnp.zeros_like(tend)))
        return jnp.concatenate(pieces, axis=0)

    def reduce(back, anal, inv):
        total = back[:rows] * anal[0:1, :]
        for k in range(1, chunks):
            total = total + back[k * rows : (k + 1) * rows] * anal[k : k + 1, :]
        result = (total[:, : 2 * waves] + total[:, 2 * waves :]) * inv
        return jnp.concatenate(
            [
                jnp.where(out_lane < waves, result, 0.0).astype(BF16),
                jnp.where(out_lane < waves, 0.0, result).astype(BF16),
                jnp.zeros((LANES - both_rows, 2 * waves), BF16),
            ],
            axis=0,
        )

    def stretch(row):
        block = jnp.broadcast_to(row, (items, wide)).astype(BF16)
        return jnp.concatenate([block] * fields, axis=0)

    def several(part, step, carry):
        seats = [step * GROUP + g for g in range(GROUP)]
        stored = [part * chunk + v for v in seats]
        locals_ = [v + reverse * (band - 1 - 2 * v) for v in stored]
        made = [prepare(v) for v in locals_]
        spreads = [pick(v) for v in seats]
        turned = [
            jnp.concatenate([x * stretch(w[2][k : k + 1, :]) for k in range(chunks)], axis=0)
            for x, w in zip(spreads, made)
        ]
        grids = [
            lax.dot_general(
                x,
                jnp.concatenate([w[4], w[5], w[4], w[5]], axis=0),
                NN,
                preferred_element_type=F32,
            )
            for x, w in zip(turned, made)
        ]
        tends = [tendency(x, v, w[0]) for x, v, w in zip(grids, locals_, made)]
        backs = [
            lax.dot_general(
                x,
                jnp.concatenate([w[4], w[5], w[5], w[4]], axis=0),
                NTD,
                preferred_element_type=F32,
            )
            for x, w in zip(tends, made)
        ]
        splits = [reduce(x, w[3], w[1]) for x, w in zip(backs, made)]
        outs = [lax.dot_general(merges, x, NTD, preferred_element_type=F32) for x in splits]
        for seat, value in zip(seats, outs):
            for w in range(local_waves):
                out_ref[w, pl.ds(seat, shards, stride=chunk), :] = value[
                    w * shards : (w + 1) * shards
                ]
        return carry

    def work(part, carry):
        @pl.when(part + LEAD < parts)
        def _():
            start_in(part + LEAD, 0)

        for away in range(1, shards):
            remote(sent_ref, land_ref, in_send, in_recv, away, part).wait_recv()
        own(sent_ref, land_ref, 0, part).wait()

        @pl.when(part >= FIRST)
        def _():
            pass_far(part - FIRST)

        @pl.when(part >= SECOND)
        def _():
            pass_near(part - SECOND)

        got = land_ref[:, span_of(part), :].astype(F32).reshape(shards * chunk, -1)
        for w in range(local_waves):
            in_ref[w] = take_lanes(got, w, both_rows)
        lax.fori_loop(0, chunk // GROUP, functools.partial(several, part), 0)
        made = join_lanes([out_ref[w] for w in range(local_waves)], both_rows).astype(BF16)
        leave_ref[:, span_of(part), :] = made.reshape(shards, chunk, -1)
        for away in range(1, shards):
            remote(leave_ref, back_ref, out_send, out_recv, away, part).start()
        own(leave_ref, back_ref, 1, part).start()
        return carry

    lax.fori_loop(0, parts, work, 0)

    def rest_far(part, carry):
        pass_far(part)
        return carry

    def rest_near(part, carry):
        pass_near(part)
        return carry

    def landed(part, carry):
        for away in range(chips):
            near(away, part).wait_recv()
        return carry

    lax.fori_loop(max(parts - FIRST, 0), parts, rest_far, 0)
    lax.fori_loop(max(parts - SECOND, 0), parts, rest_near, 0)
    lax.fori_loop(0, parts, landed, 0)

    part_span = span // 2
    start = pl.multiple_of(core * part_span, part_span)
    weights = weight_ref[:half_lat, :1]

    def give(m):
        return pltpu.make_async_remote_copy(
            src_ref=give_ref.at[m],
            dst_ref=update_ref.at[m, :, :, pl.ds(start, part_span)],
            send_sem=give_send.at[m],
            recv_sem=give_recv.at[m],
            device_id={"lev": partner},
            device_id_type=pl.DeviceIdType.MESH,
        )

    def fold(s, carry):
        for v in range(lanes // LANES):
            lane = slice(v * LANES, (v + 1) * LANES)
            north = jnp.concatenate([all_ref[s, k, :, lane] for k in range(half)], axis=0)
            south = jnp.concatenate(
                [all_ref[s, shards - 1 - k, :, lane] for k in range(half)], axis=0
            )
            north = north.astype(F32)
            south = south.astype(F32)
            even = (weights * (north + south)).astype(BF16)
            odd = (weights * (north - south)).astype(BF16)
            turned_ref[s, lane, :half_lat] = even.T
            turned_ref[s, lane, half_lat:] = odd.T
        return carry

    lax.fori_loop(0, levs, fold, 0)
    pair_rows = jnp.concatenate(
        [
            out_modes_ref[pl.ds(pl.multiple_of(r * items, items), items), :]
            for r in (lev, partner)
        ],
        axis=0,
    )

    def one(m, carry):
        seat = lax.broadcasted_iota(jnp.int32, (1, part_span), 1) + start
        leg = leg_ref[m, :, pl.ds(start, part_span)]
        kept = jnp.broadcast_to(seat % 2 == 0, leg.shape)
        none = jnp.zeros_like(leg)
        polys = jnp.concatenate([jnp.where(kept, leg, none), jnp.where(kept, none, leg)], axis=0)
        mine = pl.ds(pl.multiple_of(m * both_rows, both_rows), both_rows)
        pieces = jnp.concatenate([turned_ref[s, mine, :] for s in range(levs)], axis=0)
        values = lax.dot_general(pieces, polys, NN, preferred_element_type=F32)
        values = jnp.where(seat < all_lengths[me * local_waves + m], values, 0.0).astype(BF16)
        degree = (seat + all_ids[me * local_waves + m]).astype(F32)
        damp = 1.0 / (1.0 + depth_ref[:, :1] * degree * (degree + 1.0) / float(NT * NT))
        for c in range(channels):
            stack = jnp.concatenate(
                [
                    values[s * both_rows + c * items : s * both_rows + (c + 1) * items]
                    for s in range(levs)
                ],
                axis=0,
            )
            vals = lax.dot_general(in_modes_ref[...], stack, NN, preferred_element_type=F32)
            scaled = (vals * damp).astype(BF16)
            mixed = lax.dot_general(pair_rows, scaled, NN, preferred_element_type=F32)
            mixed = mixed.astype(BF16)
            update_ref[m, c, :, pl.ds(start, part_span)] = mixed[:items]
            give_ref[m, c] = mixed[items:]
        give(m).start()
        return carry

    lax.fori_loop(0, local_waves, one, 0)

    def finish(part, carry):
        for away in range(1, shards):
            remote(sent_ref, land_ref, in_send, in_recv, away, part).wait_send()
            remote(leave_ref, back_ref, out_send, out_recv, away, part).wait_send()
        for away in range(1, chips):
            far(away, part).wait_send()
        for away in range(chips):
            near(away, part).wait_send()
        return carry

    lax.fori_loop(0, parts, finish, 0)

    def given(m, carry):
        give(m).wait()
        return carry

    lax.fori_loop(0, local_waves, given, 0)


def on_device(
    spectral,
    legendre,
    wave_ids,
    trunc_lengths,
    cycle_points,
    grid_coef,
    cycle_weights,
    modes_in,
    modes_out,
    depths,
):
    shards = lax.axis_size("wave")
    levs = lax.axis_size("lev")
    chips = levs // 2
    waves, channels, items, span = spectral.shape
    half_lat = legendre.shape[1]
    rows = channels * items
    band = grid_coef.shape[0]
    modes = modes_in.shape[0]
    lanes = pad_to(waves * rows, LANES)
    chunk = next(c for c in (16, 8) if band % c == 0)
    stride = next(c * chunk for c in (2, 1) if band % (c * chunk) == 0)
    parts = band // chunk
    messages = (shards, band, lanes)
    vmem = pl.BlockSpec(memory_space=pltpu.VMEM)
    smem = pl.BlockSpec(memory_space=pltpu.SMEM)
    hbm = pl.BlockSpec(memory_space=pltpu.HBM)
    dma = pltpu.SemaphoreType.DMA
    return pl.pallas_call(
        functools.partial(trip_kernel, chunk, stride),
        name="trip",
        out_shape=jax.ShapeDtypeStruct(spectral.shape, BF16),
        in_specs=[smem] * 3 + [hbm] * 3 + [vmem] * 4,
        out_specs=vmem,
        scratch_shapes=[
            pltpu.VMEM(spectral.shape, BF16),
            pltpu.VMEM(legendre.shape, BF16),
            pltpu.VMEM(grid_coef.shape, F32),
            pltpu.VMEM((waves, 2 * pad_to(rows, LANES), span), BF16),
            pltpu.VMEM(messages, BF16),
            pltpu.VMEM(messages, BF16),
            pltpu.VMEM(messages, BF16),
            pltpu.VMEM((levs, *messages), BF16),
            pltpu.VMEM((waves, shards * chunk, LANES), F32),
            pltpu.VMEM((waves, shards * chunk, LANES), F32),
            pltpu.VMEM((levs, lanes, 2 * half_lat), BF16),
            pltpu.VMEM((waves, channels, items, span // 2), BF16),
            pltpu.VMEM((pad_to(half_lat, LANES), LANES), F32),
            pltpu.VMEM((modes, LANES), F32),
            dma,
            dma((band // stride, shards // 2)),
            dma,
            dma((shards - 1, parts)),
            dma((shards - 1, parts)),
            dma((shards - 1, parts)),
            dma((shards - 1, parts)),
            dma((max(chips - 1, 1), parts)),
            dma((max(chips - 1, 1), parts)),
            dma((chips, parts)),
            dma((chips, parts)),
            dma((2, parts)),
            dma((waves,)),
            dma((waves,)),
        ],
        compiler_params=pltpu.CompilerParams(
            vmem_limit_bytes=56 << 20, collective_id=0, has_side_effects=True
        ),
    )(
        wave_ids,
        trunc_lengths,
        cycle_points,
        spectral,
        legendre,
        grid_coef,
        jnp.pad(cycle_weights, (0, -half_lat % LANES)).reshape(-1, LANES),
        modes_in,
        modes_out,
        depths[None, :],
    )


def solution(mesh):
    placed = (
        P("wave", None, "lev", None),
        P("wave", None, None),
        P(),
        P(),
        P(),
        P("wave", None),
        P(),
        P(),
        P(),
        P(),
    )
    return jax.shard_map(
        on_device,
        mesh=mesh,
        in_specs=placed,
        out_specs=P("wave", None, "lev", None),
        check_vma=False,
    )
```

time: 99.9 us -> 80.5 us (0.81)
  Pallas kernels: 92.1 us -> 78 us
  local copies, waits for them, and re-layouts: 6.53 us -> 2.21 us
    pallas_call x4 -> x1, Pallas kernels: 92.1 us -> 78 us  [on_device(): pl.pallas_call(functools.partial(trip_kernel, chunk, stride), name='trip'...]
    unnamed x19 -> x1, local copies, waits for them, and re-layouts: 5.04 us -> 2.21 us
where the time goes in v1:
time: 80.5 us; the launch traced here: 80.2 us
  Pallas kernels  78 us (97%)
  local copies, waits for them, and re-layouts  2.21 us (3%)
    pallas_call x1, Pallas kernels, on_device(): pl.pallas_call(functools.partial(trip_kernel, chunk, stride), name='trip'...  78 us
    unnamed x1, local copies, waits for them, and re-layouts  2.21 us

profile of v1, /device:TPU:0, one launch (start us, length us, event | category | flops | bytes accessed | tf_op | source)
XLA Modules:
  0.0 80.2 jit_solution(12864358162680953203)
XLA Ops:
  0.0 78.0 %trip.1 = bf16[4,6,16,1280]{3,2,1,0:T(8,128)(2,1)} custom-call(s32[32]{0:T(128)} %all_ids.1, s32[32]{0:T(128)} %all_lengths.1, s32[1280]{0:T(1024)} %all_points.1, bf16[4,6,16,1280]{3,2,1,0:T(8,128)(2,1)} %spec_hbm.1, bf16[4,640,1280]{2,1,0:T(8,128)(2,1)} %leg_hbm.1, f32[160,2560]{1,0:T(8,128)} %coef_hbm.1, f32[5,128]{1,0:T(8,128)} %bitcast.2, ...), custom_call_target="tpu_custom_call" | custom-call | tf_op jit(solution)/shard_map/trip/pallas_call | solution.py:584
  78.0 2.2 %copy.12 = bf16[4,6,16,1280]{3,2,1,0:T(8,128)(2,1)} copy(bf16[4,6,16,1280]{3,2,1,0:T(8,128)(2,1)} %trip.1) | data formatting | bytes 1966080

commit v2 on v1

--- a/solution.py
+++ b/solution.py
@@ -12,9 +12,9 @@
 LOW = 256
 LANES = 128
 GROUP = 8
-LEAD = 2
-FIRST = 3
-SECOND = 5
+LEAD = 3
+FIRST = 4
+SECOND = 6
 NN = (((1,), (0,)), ((), ()))
 NTD = (((1,), (1,)), ((), ()))
 F32 = jnp.float32
@@ -447,27 +447,8 @@
 
     lax.fori_loop(0, parts, work, 0)
 
-    def rest_far(part, carry):
-        pass_far(part)
-        return carry
-
-    def rest_near(part, carry):
-        pass_near(part)
-        return carry
-
-    def landed(part, carry):
-        for away in range(chips):
-            near(away, part).wait_recv()
-        return carry
-
-    lax.fori_loop(max(parts - FIRST, 0), parts, rest_far, 0)
-    lax.fori_loop(max(parts - SECOND, 0), parts, rest_near, 0)
-    lax.fori_loop(0, parts, landed, 0)
-
     part_span = span // 2
     start = pl.multiple_of(core * part_span, part_span)
-    weights = weight_ref[:half_lat, :1]
-
     def give(m):
         return pltpu.make_async_remote_copy(
             src_ref=give_ref.at[m],
@@ -478,22 +459,55 @@
             device_id_type=pl.DeviceIdType.MESH,
         )
 
-    def fold(s, carry):
-        for v in range(lanes // LANES):
-            lane = slice(v * LANES, (v + 1) * LANES)
-            north = jnp.concatenate([all_ref[s, k, :, lane] for k in range(half)], axis=0)
-            south = jnp.concatenate(
-                [all_ref[s, shards - 1 - k, :, lane] for k in range(half)], axis=0
-            )
-            north = north.astype(F32)
-            south = south.astype(F32)
-            even = (weights * (north + south)).astype(BF16)
-            odd = (weights * (north - south)).astype(BF16)
-            turned_ref[s, lane, :half_lat] = even.T
-            turned_ref[s, lane, half_lat:] = odd.T
-        return carry
-
-    lax.fori_loop(0, levs, fold, 0)
+    def fold(part, carry):
+        for away in range(chips):
+            near(away, part).wait_recv()
+        weights = jnp.concatenate(
+            [
+                weight_ref[pl.ds(pl.multiple_of(k * band + part * chunk, 8), chunk), :]
+                for k in range(half)
+            ],
+            axis=0,
+        )
+        sides = []
+        for s in range(levs):
+            pieces = []
+            for v in range(lanes // LANES):
+                lane = slice(v * LANES, (v + 1) * LANES)
+                north, south = [
+                    jnp.concatenate([all_ref[s, k, span_of(part), lane] for k in order], axis=0)
+                    for order in (range(half), [shards - 1 - k for k in range(half)])
+                ]
+                north = north.astype(F32)
+                south = south.astype(F32)
+                even = (weights * (north + south)).astype(BF16)
+                odd = (weights * (north - south)).astype(BF16)
+                pieces.append(jnp.concatenate([even, odd], axis=0).T)
+            sides.append(jnp.concatenate(pieces, axis=0))
+        for m in range(local_waves):
+            for c in range(channels):
+                low = m * both_rows + c * items
+                stack = jnp.concatenate([side[low : low + items] for side in sides], axis=0)
+                vals = lax.dot_general(in_modes_ref[...], stack, NN, preferred_element_type=F32)
+                turned_ref[part, m, c * modes : (c + 1) * modes, :] = vals.astype(BF16)
+        return carry
+
+    def ready(turn):
+        return jnp.clip(jnp.minimum(2 * (turn + 1), parts - SECOND + turn), 0, parts)
+
+    def drain(turn, carry):
+        @pl.when((parts - FIRST + turn >= 0) & (turn < FIRST))
+        def _():
+            pass_far(parts - FIRST + turn)
+
+        @pl.when((parts - SECOND + turn >= 0) & (turn < SECOND))
+        def _():
+            pass_near(parts - SECOND + turn)
+
+        lax.fori_loop(ready(turn - 1), ready(turn), fold, 0)
+        return carry
+
+    lax.fori_loop(0, max(SECOND, -(-parts // 2) - 1) + 1, drain, 0)
     pair_rows = jnp.concatenate(
         [
             out_modes_ref[pl.ds(pl.multiple_of(r * items, items), items), :]
@@ -504,26 +518,30 @@
 
     def one(m, carry):
         seat = lax.broadcasted_iota(jnp.int32, (1, part_span), 1) + start
-        leg = leg_ref[m, :, pl.ds(start, part_span)]
-        kept = jnp.broadcast_to(seat % 2 == 0, leg.shape)
-        none = jnp.zeros_like(leg)
-        polys = jnp.concatenate([jnp.where(kept, leg, none), jnp.where(kept, none, leg)], axis=0)
-        mine = pl.ds(pl.multiple_of(m * both_rows, both_rows), both_rows)
-        pieces = jnp.concatenate([turned_ref[s, mine, :] for s in range(levs)], axis=0)
-        values = lax.dot_general(pieces, polys, NN, preferred_element_type=F32)
-        values = jnp.where(seat < all_lengths[me * local_waves + m], values, 0.0).astype(BF16)
-        degree = (seat + all_ids[me * local_waves + m]).astype(F32)
-        damp = 1.0 / (1.0 + depth_ref[:, :1] * degree * (degree + 1.0) / float(NT * NT))
-        for c in range(channels):
-            stack = jnp.concatenate(
+        polys = []
+        for p in range(parts):
+            leg = jnp.concatenate(
                 [
-                    values[s * both_rows + c * items : s * both_rows + (c + 1) * items]
-                    for s in range(levs)
+                    leg_ref[m, k * band + p * chunk : k * band + (p + 1) * chunk, pl.ds(start, part_span)]
+                    for k in range(half)
                 ],
                 axis=0,
             )
-            vals = lax.dot_general(in_modes_ref[...], stack, NN, preferred_element_type=F32)
-            scaled = (vals * damp).astype(BF16)
+            kept = jnp.broadcast_to(seat % 2 == 0, leg.shape)
+            none = jnp.zeros_like(leg)
+            polys += [jnp.where(kept, leg, none), jnp.where(kept, none, leg)]
+        values = lax.dot_general(
+            jnp.concatenate([turned_ref[p, m] for p in range(parts)], axis=1),
+            jnp.concatenate(polys, axis=0),
+            NN,
+            preferred_element_type=F32,
+        )
+        degree = (seat + all_ids[me * local_waves + m]).astype(F32)
+        live = seat < all_lengths[me * local_waves + m]
+        damp = 1.0 / (1.0 + depth_ref[:, :1] * degree * (degree + 1.0) / float(NT * NT))
+        damp = jnp.where(live, damp, 0.0)
+        for c in range(channels):
+            scaled = (values[c * modes : (c + 1) * modes] * damp).astype(BF16)
             mixed = lax.dot_general(pair_rows, scaled, NN, preferred_element_type=F32)
             mixed = mixed.astype(BF16)
             update_ref[m, c, :, pl.ds(start, part_span)] = mixed[:items]
@@ -598,7 +616,7 @@
             pltpu.VMEM((levs, *messages), BF16),
             pltpu.VMEM((waves, shards * chunk, LANES), F32),
             pltpu.VMEM((waves, shards * chunk, LANES), F32),
-            pltpu.VMEM((levs, lanes, 2 * half_lat), BF16),
+            pltpu.VMEM((parts, waves, channels * modes, shards * chunk), BF16),
             pltpu.VMEM((waves, channels, items, span // 2), BF16),
             pltpu.VMEM((pad_to(half_lat, LANES), LANES), F32),
             pltpu.VMEM((modes, LANES), F32),

time: 80.5 us -> 72.7 us (0.903)
  Pallas kernels: 78 us -> 70.3 us
    pallas_call x1, Pallas kernels: 78 us -> 70.3 us  [on_device(): pl.pallas_call(functools.partial(trip_kernel, chunk, stride), name='trip'...]
where the time goes in v2:
time: 72.7 us; the launch traced here: 72.5 us
  Pallas kernels  70.3 us (97%)
  local copies, waits for them, and re-layouts  2.21 us (3%)
    pallas_call x1, Pallas kernels, on_device(): pl.pallas_call(functools.partial(trip_kernel, chunk, stride), name='trip'...  70.3 us
    unnamed x1, local copies, waits for them, and re-layouts  2.21 us

profile of v2, /device:TPU:0, one launch (start us, length us, event | category | flops | bytes accessed | tf_op | source)
XLA Modules:
  0.0 72.5 jit_solution(15456157430875044994)
XLA Ops:
  0.0 70.3 %trip.1 = bf16[4,6,16,1280]{3,2,1,0:T(8,128)(2,1)} custom-call(s32[32]{0:T(128)} %all_ids.1, s32[32]{0:T(128)} %all_lengths.1, s32[1280]{0:T(1024)} %all_points.1, bf16[4,6,16,1280]{3,2,1,0:T(8,128)(2,1)} %spec_hbm.1, bf16[4,640,1280]{2,1,0:T(8,128)(2,1)} %leg_hbm.1, f32[160,2560]{1,0:T(8,128)} %coef_hbm.1, f32[5,128]{1,0:T(8,128)} %bitcast.2, ...), custom_call_target="tpu_custom_call" | custom-call | tf_op jit(solution)/shard_map/trip/pallas_call | solution.py:602
  70.3 2.2 %copy.12 = bf16[4,6,16,1280]{3,2,1,0:T(8,128)(2,1)} copy(bf16[4,6,16,1280]{3,2,1,0:T(8,128)(2,1)} %trip.1) | data formatting | bytes 1966080

commit v3 on v2

--- a/solution.py
+++ b/solution.py
@@ -15,6 +15,7 @@
 LEAD = 3
 FIRST = 4
 SECOND = 6
+THIRD = 10
 NN = (((1,), (0,)), ((), ()))
 NTD = (((1,), (1,)), ((), ()))
 F32 = jnp.float32
@@ -96,6 +97,7 @@
     give_ref,
     weight_ref,
     depth_ref,
+    acc_ref,
     spec_sem,
     leg_sems,
     coef_sem,
@@ -141,7 +143,7 @@
     def leg_copy(step, k):
         where = pl.ds(pl.multiple_of(k * band + step * stride, 8), stride)
         return pltpu.make_async_copy(
-            leg_hbm.at[:, where, :], leg_ref.at[:, where, :], leg_sems.at[step, k]
+            leg_hbm.at[:, where, :], leg_ref.at[:, where, :], leg_sems.at[step]
         )
 
     spec_copy.start()
@@ -175,9 +177,31 @@
         return pltpu.make_async_remote_copy(
             src_ref=src.at[to, span_of(part), :],
             dst_ref=dst.at[me, span_of(part), :],
-            send_sem=send.at[away - 1, part],
-            recv_sem=recv.at[away - 1, part],
+            send_sem=send,
+            recv_sem=recv.at[part],
             device_id={"wave": to},
+            device_id_type=pl.DeviceIdType.MESH,
+        )
+
+    def arrived(dst, send, recv, part):
+        block = dst.at[pl.ds(0, shards - 1), span_of(part), :]
+        return pltpu.make_async_remote_copy(
+            src_ref=block,
+            dst_ref=block,
+            send_sem=send,
+            recv_sem=recv.at[part],
+            device_id={"wave": lax.rem(me + 1, shards)},
+            device_id_type=pl.DeviceIdType.MESH,
+        )
+
+    def departed(src, send, recv):
+        block = src.at[pl.ds(0, shards - 1)]
+        return pltpu.make_async_remote_copy(
+            src_ref=block,
+            dst_ref=block,
+            send_sem=send,
+            recv_sem=recv.at[0],
+            device_id={"wave": lax.rem(me + 1, shards)},
             device_id_type=pl.DeviceIdType.MESH,
         )
 
@@ -212,8 +236,7 @@
         )
 
     def pass_far(part):
-        for away in range(1, shards):
-            remote(leave_ref, back_ref, out_send, out_recv, away, part).wait_recv()
+        arrived(back_ref, out_send, out_recv, part).wait_recv()
         own(leave_ref, back_ref, 1, part).wait()
         for away in range(1, chips):
             far(away, part).start()
@@ -240,8 +263,8 @@
         both_ref[m] = jnp.concatenate([live.astype(BF16), fill, sign, fill], axis=0)
 
     def inverse(step):
-        for k in range(half):
-            leg_copy(step, k).wait()
+        taken = leg_ref.at[:, pl.ds(0, half * stride), :]
+        pltpu.make_async_copy(taken, taken, leg_sems.at[step]).wait()
         north, south = [], []
         for m in range(local_waves):
             polys = jnp.concatenate(
@@ -417,48 +440,6 @@
                 ]
         return carry
 
-    def work(part, carry):
-        @pl.when(part + LEAD < parts)
-        def _():
-            start_in(part + LEAD, 0)
-
-        for away in range(1, shards):
-            remote(sent_ref, land_ref, in_send, in_recv, away, part).wait_recv()
-        own(sent_ref, land_ref, 0, part).wait()
-
-        @pl.when(part >= FIRST)
-        def _():
-            pass_far(part - FIRST)
-
-        @pl.when(part >= SECOND)
-        def _():
-            pass_near(part - SECOND)
-
-        got = land_ref[:, span_of(part), :].astype(F32).reshape(shards * chunk, -1)
-        for w in range(local_waves):
-            in_ref[w] = take_lanes(got, w, both_rows)
-        lax.fori_loop(0, chunk // GROUP, functools.partial(several, part), 0)
-        made = join_lanes([out_ref[w] for w in range(local_waves)], both_rows).astype(BF16)
-        leave_ref[:, span_of(part), :] = made.reshape(shards, chunk, -1)
-        for away in range(1, shards):
-            remote(leave_ref, back_ref, out_send, out_recv, away, part).start()
-        own(leave_ref, back_ref, 1, part).start()
-        return carry
-
-    lax.fori_loop(0, parts, work, 0)
-
-    part_span = span // 2
-    start = pl.multiple_of(core * part_span, part_span)
-    def give(m):
-        return pltpu.make_async_remote_copy(
-            src_ref=give_ref.at[m],
-            dst_ref=update_ref.at[m, :, :, pl.ds(start, part_span)],
-            send_sem=give_send.at[m],
-            recv_sem=give_recv.at[m],
-            device_id={"lev": partner},
-            device_id_type=pl.DeviceIdType.MESH,
-        )
-
     def fold(part, carry):
         for away in range(chips):
             near(away, part).wait_recv()
@@ -492,8 +473,83 @@
                 turned_ref[part, m, c * modes : (c + 1) * modes, :] = vals.astype(BF16)
         return carry
 
+    def work(part, carry):
+        @pl.when(part + LEAD < parts)
+        def _():
+            start_in(part + LEAD, 0)
+
+        arrived(land_ref, in_send, in_recv, part).wait_recv()
+        own(sent_ref, land_ref, 0, part).wait()
+
+        @pl.when(part >= FIRST)
+        def _():
+            pass_far(part - FIRST)
+
+        @pl.when(part >= SECOND)
+        def _():
+            pass_near(part - SECOND)
+
+        got = land_ref[:, span_of(part), :].astype(F32).reshape(shards * chunk, -1)
+        for w in range(local_waves):
+            in_ref[w] = take_lanes(got, w, both_rows)
+        lax.fori_loop(0, chunk // GROUP, functools.partial(several, part), 0)
+        made = join_lanes([out_ref[w] for w in range(local_waves)], both_rows).astype(BF16)
+        leave_ref[:, span_of(part), :] = made.reshape(shards, chunk, -1)
+        for away in range(1, shards):
+            remote(leave_ref, back_ref, out_send, out_recv, away, part).start()
+        own(leave_ref, back_ref, 1, part).start()
+
+        @pl.when(part >= THIRD)
+        def _():
+            fold(part - THIRD, 0)
+
+        return carry
+
+    lax.fori_loop(0, parts, work, 0)
+
+    def give(m):
+        return pltpu.make_async_remote_copy(
+            src_ref=give_ref.at[m],
+            dst_ref=update_ref.at[m, :, :, pl.ds(start, part_span)],
+            send_sem=give_send.at[m],
+            recv_sem=give_recv.at[m],
+            device_id={"lev": partner},
+            device_id_type=pl.DeviceIdType.MESH,
+        )
+
+    part_span = span // 2
+    start = pl.multiple_of(core * part_span, part_span)
+    folded = max(parts - THIRD, 0)
+    early = max(parts - SECOND + 2, 0)
+
+    def forward(m, first, last):
+        seat = lax.broadcasted_iota(jnp.int32, (1, part_span), 1) + start
+        polys = []
+        for p in range(first, last):
+            leg = jnp.concatenate(
+                [
+                    leg_ref[m, pl.ds(k * band + p * chunk, chunk), pl.ds(start, part_span)]
+                    for k in range(half)
+                ],
+                axis=0,
+            )
+            kept = jnp.broadcast_to(seat % 2 == 0, leg.shape)
+            none = jnp.zeros_like(leg)
+            polys += [jnp.where(kept, leg, none), jnp.where(kept, none, leg)]
+        return lax.dot_general(
+            jnp.concatenate([turned_ref[p, m] for p in range(first, last)], axis=1),
+            jnp.concatenate(polys, axis=0),
+            NN,
+            preferred_element_type=F32,
+        )
+
+    def head(m, carry):
+        acc_ref[m] = forward(m, 0, early)
+        return carry
+
     def ready(turn):
-        return jnp.clip(jnp.minimum(2 * (turn + 1), parts - SECOND + turn), 0, parts)
+        done = jnp.minimum(folded + 2 * (turn + 1), parts - SECOND + turn)
+        return jnp.clip(done, folded, parts)
 
     def drain(turn, carry):
         @pl.when((parts - FIRST + turn >= 0) & (turn < FIRST))
@@ -504,10 +560,19 @@
         def _():
             pass_near(parts - SECOND + turn)
 
+        if early:
+
+            @pl.when((turn >= 3) & (turn - 3 < local_waves))
+            def _():
+                head(turn - 3, 0)
+
         lax.fori_loop(ready(turn - 1), ready(turn), fold, 0)
         return carry
 
-    lax.fori_loop(0, max(SECOND, -(-parts // 2) - 1) + 1, drain, 0)
+    turns_left = max(SECOND, -(-(parts - folded) // 2) - 1) + 1
+    lax.fori_loop(0, turns_left, drain, 0)
+    if early:
+        lax.fori_loop(min(turns_left - 3, local_waves), local_waves, head, 0)
     pair_rows = jnp.concatenate(
         [
             out_modes_ref[pl.ds(pl.multiple_of(r * items, items), items), :]
@@ -518,24 +583,9 @@
 
     def one(m, carry):
         seat = lax.broadcasted_iota(jnp.int32, (1, part_span), 1) + start
-        polys = []
-        for p in range(parts):
-            leg = jnp.concatenate(
-                [
-                    leg_ref[m, k * band + p * chunk : k * band + (p + 1) * chunk, pl.ds(start, part_span)]
-                    for k in range(half)
-                ],
-                axis=0,
-            )
-            kept = jnp.broadcast_to(seat % 2 == 0, leg.shape)
-            none = jnp.zeros_like(leg)
-            polys += [jnp.where(kept, leg, none), jnp.where(kept, none, leg)]
-        values = lax.dot_general(
-            jnp.concatenate([turned_ref[p, m] for p in range(parts)], axis=1),
-            jnp.concatenate(polys, axis=0),
-            NN,
-            preferred_element_type=F32,
-        )
+        values = forward(m, early, parts)
+        if early:
+            values = values + acc_ref[m]
         degree = (seat + all_ids[me * local_waves + m]).astype(F32)
         live = seat < all_lengths[me * local_waves + m]
         damp = 1.0 / (1.0 + depth_ref[:, :1] * degree * (degree + 1.0) / float(NT * NT))
@@ -551,10 +601,10 @@
 
     lax.fori_loop(0, local_waves, one, 0)
 
+    departed(sent_ref, in_send, in_recv).wait_send()
+    departed(leave_ref, out_send, out_recv).wait_send()
+
     def finish(part, carry):
-        for away in range(1, shards):
-            remote(sent_ref, land_ref, in_send, in_recv, away, part).wait_send()
-            remote(leave_ref, back_ref, out_send, out_recv, away, part).wait_send()
         for away in range(1, chips):
             far(away, part).wait_send()
         for away in range(chips):
@@ -620,13 +670,14 @@
             pltpu.VMEM((waves, channels, items, span // 2), BF16),
             pltpu.VMEM((pad_to(half_lat, LANES), LANES), F32),
             pltpu.VMEM((modes, LANES), F32),
+            pltpu.VMEM((waves, channels * modes, span // 2), F32),
             dma,
-            dma((band // stride, shards // 2)),
+            dma((band // stride,)),
             dma,
-            dma((shards - 1, parts)),
-            dma((shards - 1, parts)),
-            dma((shards - 1, parts)),
-            dma((shards - 1, parts)),
+            dma,
+            dma((parts,)),
+            dma,
+            dma((parts,)),
             dma((max(chips - 1, 1), parts)),
             dma((max(chips - 1, 1), parts)),
             dma((chips, parts)),

time: 72.7 us -> 68.5 us (0.942)
  Pallas kernels: 70.3 us -> 66.1 us
    pallas_call x1, Pallas kernels: 70.3 us -> 66.1 us  [on_device(): pl.pallas_call(functools.partial(trip_kernel, chunk, stride), name='trip'...]
where the time goes in v3:
time: 68.5 us; the launch traced here: 68.3 us
  Pallas kernels  66.1 us (96%)
  local copies, waits for them, and re-layouts  2.21 us (3%)
    pallas_call x1, Pallas kernels, on_device(): pl.pallas_call(functools.partial(trip_kernel, chunk, stride), name='trip'...  66.1 us
    unnamed x1, local copies, waits for them, and re-layouts  2.21 us

profile of v3, /device:TPU:0, one launch (start us, length us, event | category | flops | bytes accessed | tf_op | source)
XLA Modules:
  0.0 68.3 jit_solution(4850689033905505300)
XLA Ops:
  0.0 66.1 %trip.1 = bf16[4,6,16,1280]{3,2,1,0:T(8,128)(2,1)} custom-call(s32[32]{0:T(128)} %all_ids.1, s32[32]{0:T(128)} %all_lengths.1, s32[1280]{0:T(1024)} %all_points.1, bf16[4,6,16,1280]{3,2,1,0:T(8,128)(2,1)} %spec_hbm.1, bf16[4,640,1280]{2,1,0:T(8,128)(2,1)} %leg_hbm.1, f32[160,2560]{1,0:T(8,128)} %coef_hbm.1, f32[5,128]{1,0:T(8,128)} %bitcast.2, ...), custom_call_target="tpu_custom_call" | custom-call | tf_op jit(solution)/shard_map/trip/pallas_call | solution.py:652
  66.1 2.2 %copy.12 = bf16[4,6,16,1280]{3,2,1,0:T(8,128)(2,1)} copy(bf16[4,6,16,1280]{3,2,1,0:T(8,128)(2,1)} %trip.1) | data formatting | bytes 1966080
